TPU v7x, 32 devices: a 4x4x1 block of a 4x4x8 slice. The times are simulated.
32 devices in a mesh: dp: 1 (over z), ri: 4 (over y), co: 4 (over x), ro: 2 (over core).
Axes of the slice: x: 4, y: 4, z: 1, core: 2. Of those that a mesh axis runs over, the one named last changes fastest.
The devices are a block of a 4x4x8 slice.
Arguments:
- act_in: bfloat16 [32768, 5120], P(('dp', 'ro', 'ri'), 'co')
- weight: bfloat16 [5120, 5120], P(('ro', 'ri'), 'co')
Outputs:
- output: bfloat16 [32768, 5120], P(('dp', 'ro', 'ri', 'co'))
All inputs are finite; a program needn't handle non-finite values.
Results may differ from a plain program's by a relative error of at most 0.001.
Values are sent between devices in bfloat16 or wider.
A program may use at most 768 MiB of HBM per device.

v0:
```python
import jax
import jax.numpy as jnp
from jax import lax
from jax.sharding import PartitionSpec as P


def solution(mesh):
    def local_block(act_blk, weight_blk):
        act_rows = lax.all_gather(act_blk, "co", axis=1, tiled=True)
        weight_cols = lax.all_gather(weight_blk, ("ro", "ri"), axis=0, tiled=True)
        block_out = jnp.dot(act_rows, weight_cols, preferred_element_type=jnp.float32).astype(jnp.bfloat16)
        return lax.all_to_all(block_out, "co", 0, 1, tiled=True)

    return jax.shard_map(
        local_block,
        mesh=mesh,
        in_specs=(P(("dp", "ro", "ri"), "co"), P(("ro", "ri"), "co")),
        out_specs=P(("dp", "ro", "ri", "co"), None),
        check_vma=False,
    )
```

profile of v0, /device:TPU:97, one launch (start us, length us, event | category | flops | bytes accessed | tf_op | source)
XLA Modules:
  0.0 641.2 jit_solution(1847612971054608342)
XLA Ops:
  6.5 0.0 all-gather.5.cloned.1.call-start
  6.6 0.7 all-gather.5.cloned.1.call-update
  7.3 0.1 all-gather.3.cloned.1.call-start
  7.4 0.7 all-gather.3.cloned.1.call-update
  8.1 72.3 %all-gather.5.cloned.1.call-done = bf16[5120,1280]{1,0:T(8,128)(2,1)} async-done(((bf16[640,1280]{1,0:T(8,128)(2,1)}), bf16[5120,1280]{1,0:T(8,128)(2,1)}) %all-gather.5.cloned.1.call-update) | async-done | bytes 13107216 | tf_op jit(solution)/shard_map/all_gather | solution.py:10
  80.4 362.7 %all-gather.3.cloned.1.call-done = bf16[4096,5120]{1,0:T(8,128)(2,1)} async-done(((bf16[4096,1280]{1,0:T(8,128)(2,1)}), bf16[4096,5120]{1,0:T(8,128)(2,1)}) %all-gather.3.cloned.1.call-update) | async-done | bytes 41943056 | tf_op jit(solution)/shard_map/all_gather | solution.py:9
  443.1 62.4 %convolution_convert_fusion = bf16[4096,1280]{1,0:T(8,128)(2,1)S(1)} fusion(bf16[4096,5120]{1,0:T(8,128)(2,1)} %all-gather.3.cloned.1.call-done, bf16[5120,1280]{1,0:T(8,128)(2,1)} %all-gather.5.cloned.1.call-done), kind=kOutput, calls=%fused_computation | convolution fusion | flops 53692334080 | bytes 65536000 | tf_op jit(solution)/shard_map/dot_general | solution.py:11
  505.5 119.3 %all_to_all.19 = bf16[4,1024,1280]{2,1,0:T(8,128)(2,1)} all-to-all(bf16[4,1024,1280]{2,1,0:T(8,128)(2,1)S(1)} %bitcast.7), channel_id=1, replica_groups=mesh['dp'=1,'ri'=4,'co'=4,'ro'=2] {'co'}, dimensions={0} | all-to-all | bytes 20971520 | tf_op jit(solution)/shard_map/all_to_all | solution.py:12
  624.8 9.5 %copy.4 = bf16[4,128,8,1280]{3,2,0,1:T(8,128)(2,1)} copy(bf16[4,128,8,1280]{3,2,1,0:T(8,128)(2,1)} %bitcast.6) | data formatting | bytes 20971520 | tf_op jit(solution)/shard_map/all_to_all | solution.py:12
Async XLA Ops:
  6.5 73.8 %all-gather.5.cloned.1.call-start = ((), (), s32[]{:S(2)}) async-start(), calls=%async_computation.2 | async-start | bytes 14745600 | tf_op jit(solution)/shard_map/all_gather | solution.py:10
  7.3 435.8 %all-gather.3.cloned.1.call-start = ((), (), s32[]{:S(2)}) async-start(), calls=%async_computation.1 | async-start | bytes 52428800 | tf_op jit(solution)/shard_map/all_gather | solution.py:9
Sparse Core Ops, SparseCore 0:
  9.0 71.3 all-gather.4
  82.0 361.1 all-gather.2
where the time goes:
time: 641 us
  waiting for transfers between devices  436 us (68%)
  blocking collectives  119 us (19%)
  matrix products  62.4 us (10%)
  between operations  13.4 us (2%)
  local copies, waits for them, and re-layouts  9.52 us (1%)
    all_gather x1, waiting for transfers between devices, local_block(): act_rows = lax.all_gather(act_blk, 'co', axis=1, tiled=True)  363 us
    all_to_all x1, blocking collectives, local_block(): return lax.all_to_all(block_out, 'co', 0, 1, tiled=True)  119 us
    all_gather x1, waiting for transfers between devices, local_block(): weight_cols = lax.all_gather(weight_blk, ('ro', 'ri'), axis=0, tiled=True)  72.3 us
    dot_general x1, matrix products, local_block(): jnp.dot(act_rows, weight_cols, preferred_element_type=jnp.float32)  62.4 us
  transfers between devices with their start and end apart: 2, of which 2 were waited for; matrix products, arithmetic and copies ran while one was open for 0% of the time, Pallas kernels for 0%

commit v1 on v0

v1 whole, which is shorter than its diff:
```python
import functools

import jax
import jax.numpy as jnp
from jax import lax
from jax.experimental import pallas as pl
from jax.experimental.pallas import tpu as pltpu
from jax.sharding import PartitionSpec as P

MESH = pl.DeviceIdType.MESH
VMEM = 48 * 1024 * 1024
PARTS = 5
FIRST = 3
PIECES = ((0, FIRST), (FIRST, PARTS))

_NEAR = [
    [(0, 0)], [(0, -1)], [(1, -1)], [(2, 0)], [(2, -1)], [(0, 1), (2, 1)], [(0, 2), (2, 2)], [(-1, -1)],
    [(1, 0), (-1, 0)], [(1, 2), (-1, 2)], [(1, 1), (-1, 1)],
]
_FAR = [
    [(1, 0)], [(1, -1)], [(0, -1)], [(-1, 0)], [(-1, -1)], [(1, 1), (-1, 1)], [(1, 2), (-1, 2)], [(2, -1)],
    [(0, 0), (2, 0)], [(0, 2), (2, 2)], [(0, 1), (2, 1)],
]
_FINAL = (21, 23, 25, 27, 28, 29, 30, 31)

_EVENTS = [((-1, 0), 0), ((1, 0), 0), ((0, -1), 0), ((0, 1), 0), ((-1, 0), 1), ((1, 0), 1), ((0, -1), 1), ((0, 1), 1), ((-1, -1), 0), ((-1, 1), 0), ('T', 0), ((-1, -1), 1), ((-1, 1), 1), ('T', 1), ((-1, 2), 0), ((1, 1), 0), ('L', 0), ((2, 0), 0), ((-1, 2), 1), ((1, 1), 1), ((2, 0), 1), ('U', 0), ((1, -1), 0), ((2, 1), 0), ('E', 0), ('U', 1), ((1, -1), 1), ((2, 1), 1), ((2, -1), 0), ((2, -1), 1), ('Z', 0), ((0, 2), 0), ((2, 2), 0), ((0, 2), 1), ((1, 2), 0), ((2, 2), 1), ((1, 2), 1)]
_COUNTS = [17, 0, 0, 0, 0, 3, 6, 0, 2, 0, 0, 0, 0, 1, 0, 0, 1, 0, 1, 0, 1, 0, 2, 0, 0, 0, 2, 1, 0, 0, 0, 0]
_FRESH = (0, 5, 6, 16, 18, 20, 22, 26)


def order(table):
    return [(k, i, h) for row in table for h in range(2) for k, i in row]


def plan():
    events = _EVENTS
    out = []
    for count in _COUNTS:
        out.append(events[:count])
        events = events[count:]
    assert not events
    return out


def sends(event, near):
    what, h = event
    out = []
    if what in ("T", "U"):
        out = [("x", 1, "F", h)]
        if h and not near:
            out += [("x", 1, "T", 0), ("x", 1, "T", 1), ("x", 1, "H", 0)]
        if h and near:
            out += [("x", 1, (-1, 2), q) for q in range(2)]
    if isinstance(what, str):
        return out
    if what == (-1, 0):
        if not near:
            out = [("x", 1, what, h)]
        out += [("y", 1, what, h), ("y", -1, what, h)]
        if h and near:
            out += [("x", 1, "T", 0), ("x", 1, "T", 1), ("x", 1, what, 0), ("x", 1, what, 1), ("x", 1, "H", 0)]
    if what == (-1, 2) and not near:
        out = [("x", 1, what, h)]
    if what == (1, 0) and h:
        out = [("y", -1, what, q) for q in range(2)]
    if what == (2, 0):
        out = [("y", -1, what, h)]
        if h:
            out += [("y", 1, b, q) for b in ((2, 0), (0, -1)) for q in range(2)]
    if what == (-1, -1):
        out = [("y", 1, what, h)]
        if h:
            out += [("y", 1, b, q) for b in ((1, 0),) for q in range(2)]
    if what == (1, -1) and h == 0:
        out = [("y", 1, what, h)]
    if what == (0, 2) and h == 1:
        out = [("x", -1, what, h)]
    return out + [("c", 1, what, h)]


def first_sends():
    own = (0, 0)
    out = [(axis, s, own, h) for h in range(2) for s in (1, -1) for axis in "xy"]
    return out + [("x", -1, "L", 0)] + [("c", 1, own, h) for h in range(2)]


def kernel(nx, ny, a_ref, b_ref, o_ref, bg, av, transit, acc, bbuf,
           a_load, b_load, load_sem, recv_b, recv_a, send_sem):
    x, y, c = lax.axis_index("co"), lax.axis_index("ri"), lax.axis_index("ro")
    d = 1 - 2 * c
    xs = lambda i: lax.rem(x + i * d + 2 * nx, nx)
    ys = lambda j: lax.rem(y + j * d + 2 * ny, ny)
    target = lambda axis, s: {"co": xs(s)} if axis == "x" else {"ri": ys(s)} if axis == "y" else {"ro": 1 - c}
    rows, (kb, nb) = av.shape[1], b_ref.shape
    part, half = nb // PARTS, rows // 2

    barrier = pltpu.get_barrier_semaphore()
    for who in (target("x", 1), target("x", -1), target("y", 1), target("y", -1), target("c", 1)):
        pl.semaphore_signal(barrier, inc=1, device_id=who, device_id_type=MESH)
    pl.semaphore_wait(barrier, 5)

    def cols(h):
        first, last = PIECES[h]
        return pl.ds(first * part, (last - first) * part)

    def row_of(j):
        return c * ny + ys(j)

    def piece(r, n, h):
        return bg.at[r, n, :, cols(h)]

    def a_rows(s, first, count):
        return a_ref.at[pl.ds(pl.multiple_of(xs(s) * rows + first, half), count)]

    sent = []

    def push(send):
        axis, s, what, h = send
        if send not in sent:
            sent.append(send)
        index = sent.index(send)
        if isinstance(what, str):
            at = pl.ds(h * half, half)
            if what == "L":
                src, dst, recv = a_rows(-1, 0, rows), av.at[x], 0
            elif what == "H":
                src, dst, recv = a_rows(1, 0, rows), av.at[x], 1
            elif what == "T":
                src, dst, recv = a_rows(2, h * half, half), transit.at[h], 2 + h
            else:
                src, dst, recv = transit.at[h], av.at[xs(-1), at], 4 + h
            sems = send_sem.at[index], recv_a.at[recv]
        else:
            i, j = what
            r, n = row_of(j), xs(i)
            dst = piece(r, n, h)
            src = b_ref.at[:, cols(h)] if what == (0, 0) else dst
            sems = send_sem.at[index], recv_b.at[r, n, h]
        pltpu.make_async_remote_copy(
            src_ref=src, dst_ref=dst, send_sem=sems[0], recv_sem=sems[1],
            device_id=target(axis, s), device_id_type=MESH).start()

    def wait(ref, sem):
        pltpu.make_async_copy(ref, ref, sem).wait()

    def wait_b(r, n, h):
        wait(piece(r, n, h), recv_b.at[r, n, h])

    near = lax.rem(x, 2) == lax.div(y, 2)

    def only(want, action):
        pl.when(near if want else jnp.logical_not(near))(action)

    def wait_behind():
        wait(av.at[xs(-1)], recv_a.at[1])

    def wait_across():
        for q in range(2):
            wait(av.at[xs(2), pl.ds(q * half, half)], recv_a.at[4 + q])

    def handle(event):
        what, h = event
        if what in ("T", "U"):
            @functools.partial(only, what == "U")
            def _():
                wait(transit.at[h], recv_a.at[2 + h])
                for send in sends(event, what == "U"):
                    push(send)
            return
        if what == "L":
            wait(av.at[xs(1)], recv_a.at[0])
        elif what in ("E", "Z"):
            only(what == "E", wait_across)
            only(what == "Z", wait_behind)
        else:
            i, j = what
            wait_b(row_of(j), xs(i), h)
        both = [sends(event, want) for want in (False, True)]
        if both[0] == both[1]:
            for send in both[0]:
                push(send)
        else:
            for want in range(2):
                @functools.partial(only, want)
                def _():
                    for send in both[want]:
                        push(send)

    for send in first_sends():
        push(send)
    own_a = pltpu.make_async_copy(a_rows(0, 0, rows), av.at[x], a_load)
    own_a.start()
    own_b = [
        pltpu.make_async_copy(b_ref.at[:, cols(h)], bbuf.at[h, pl.ds(0, kb), pl.ds(0, cols(h).size)], b_load.at[h])
        for h in range(2)]
    for copy in own_b:
        copy.start()
    back = []
    for h in range(2):
        own_b[h].wait()
        back.append(pltpu.make_async_copy(
            bbuf.at[h, pl.ds(0, kb), pl.ds(0, cols(h).size)], piece(row_of(0), x, h), b_load.at[h]))
        back[h].start()

    def clear(n, _):
        acc[n] = jnp.zeros(acc.shape[1:], acc.dtype)
        return 0

    lax.fori_loop(0, acc.shape[0], clear, 0)
    for copy in back:
        copy.wait()
    own_a.wait()

    codes = [[(k + 1) * 8 + (i + 1) * 2 + h for k, i, h in order(t)] for t in (_NEAR, _FAR)]
    per = 6
    pack = lambda t, w: sum(v * 32 ** n for n, v in enumerate(t[w * per:(w + 1) * per]))
    words = [jnp.where(near, pack(codes[0], w), pack(codes[1], w)) for w in range(-(-len(codes[0]) // per))]

    def unit(s):
        w, m = lax.div(s, per), lax.rem(s, per)
        word = words[0]
        for n in range(1, len(words)):
            word = jnp.where(w == n, words[n], word)
        code = lax.rem(word, 32)
        for n in range(1, per):
            code = jnp.where(m == n, lax.rem(lax.div(word, 32 ** n), 32), code)
        k = xs(lax.div(code, 8) - 1)
        ro = lax.div(k, nx // 2)
        n = lax.rem(x + (lax.div(lax.rem(code, 8), 2) - 1) * (1 - 2 * ro) + 2 * nx, nx)
        return k, ro, n, lax.rem(code, 2)

    def fetch(s, what, start):
        k, ro, n, h = what
        p = lax.rem(s, 2)
        for hh in range(2):
            @pl.when(h == hh)
            def _():
                for q in range(2):
                    r = 2 * k + q
                    copy = pltpu.make_async_copy(
                        piece(r, n, hh), bbuf.at[p, pl.ds(q * kb, kb), pl.ds(0, cols(hh).size)], load_sem.at[p, q])
                    if start:
                        @pl.when(ro != c)
                        def _():
                            wait_b(r, n, hh)
                        copy.start()
                    else:
                        copy.wait()

    steps = plan()
    ahead = [t for t in range(1, len(steps)) if t not in _FRESH]

    def is_in(s, those):
        hit = s == -1
        for t in those:
            hit = jnp.logical_or(hit, s == t)
        return hit

    def step(s, this):
        for t, events in enumerate(steps):
            if events:
                @pl.when(s == t)
                def _():
                    for event in events:
                        handle(event)

        @pl.when(jnp.logical_not(is_in(s, ahead)))
        def _():
            fetch(s, this, True)

        after = unit(s + 1)

        @pl.when(is_in(s + 1, ahead))
        def _():
            fetch(s + 1, after, True)

        fetch(s, this, False)
        k, _, n, h = this
        p = lax.rem(s, 2)
        final = is_in(s, _FINAL)
        for hh, (first, last) in enumerate(PIECES):
            @pl.when(h == hh)
            def _():
                for g in range(first, last):
                    col = n * PARTS + g
                    acc[col] += jnp.dot(
                        av[k], bbuf[p, :, pl.ds((g - first) * part, part)], preferred_element_type=jnp.float32)

                @pl.when(final)
                def _():
                    for g in range(first, last):
                        col = n * PARTS + g
                        o_ref[:, pl.ds(pl.multiple_of(col * part, part), part)] = acc[col].astype(o_ref.dtype)
        return after

    lax.fori_loop(0, len(steps), step, unit(0))
    for n, (_, _, what, h) in enumerate(sent):
        ref = piece(0, 0, h) if not isinstance(what, str) else av.at[0] if what in "LH" else transit.at[0]
        wait(ref, send_sem.at[n])


def solution(mesh):
    nx, ny, nc = mesh.shape["co"], mesh.shape["ri"], mesh.shape["ro"]

    def local_block(a, b):
        rows, (kb, nb) = a.shape[0] // nx, b.shape
        kd, part = a.shape[1], nb // PARTS
        dma = pltpu.SemaphoreType.DMA
        all_sends = set(first_sends())
        for event in sum(plan(), []):
            for near in range(2):
                all_sends.update(sends(event, near))
        out, _ = pl.pallas_call(
            functools.partial(kernel, nx, ny),
            out_shape=(
                pltpu.VMEM((rows, nx * nb), jnp.bfloat16),
                jax.ShapeDtypeStruct((nc * ny, nx, kb, nb), jnp.bfloat16),
            ),
            in_specs=[pl.BlockSpec(memory_space=pl.ANY)] * 2,
            out_specs=(pl.BlockSpec(memory_space=pltpu.VMEM), pl.BlockSpec(memory_space=pl.ANY)),
            scratch_shapes=[
                pltpu.VMEM((nx, rows, kd), jnp.bfloat16),
                pltpu.VMEM((2, rows // 2, kd), jnp.bfloat16),
                pltpu.VMEM((nx * PARTS, rows, part), jnp.float32),
                pltpu.VMEM((2, 2 * kb, FIRST * part), jnp.bfloat16),
                dma, dma((2,)), dma((2, 2)),
                dma((nc * ny, nx, 2)), dma((6,)), dma((len(all_sends),)),
            ],
            compiler_params=pltpu.CompilerParams(
                collective_id=0, has_side_effects=True, vmem_limit_bytes=VMEM),
        )(a, b)
        return out

    return jax.shard_map(
        local_block,
        mesh=mesh,
        in_specs=(P(("dp", "ro", "ri"), "co"), P(("ro", "ri"), "co")),
        out_specs=P(("dp", "ro", "ri", "co"), None),
        check_vma=False,
    )
```

time: 641 us -> 223 us (0.35)
  waiting for transfers between devices: 436 us -> 0 us
  Pallas kernels: 0 us -> 216 us
  blocking collectives: 119 us -> 0 us
  matrix products: 62.4 us -> 0 us
  between operations: 13.4 us -> 0.01 us
    all_gather x2 -> x0, waiting for transfers between devices: 435 us -> none  [the longest x1 363 us: local_block(): act_rows = lax.all_gather(act_blk, 'co', axis=1, tiled=True)]
    pallas_call x0 -> x1, Pallas kernels: none -> 216 us  [local_block(): pl.pallas_call(functools.partial(kernel, nx, ny), out_shape=(pltpu.VMEM((...]
    all_to_all x1 -> x0, blocking collectives: 119 us -> none  [local_block(): return lax.all_to_all(block_out, 'co', 0, 1, tiled=True)]
    dot_general x1 -> x0, matrix products: 62.4 us -> none  [local_block(): jnp.dot(act_rows, weight_cols, preferred_element_type=jnp.float32)]
    all_to_all x1 -> x0, local copies, waits for them, and re-layouts: 9.52 us -> none  [local_block(): return lax.all_to_all(block_out, 'co', 0, 1, tiled=True)]
  transfers between devices with their start and end apart: 2 -> 0, of which waited for: 2 -> 0; matrix products, arithmetic and copies ran while one was open for 0% -> 0% of each run, Pallas kernels for 0% -> 0%
where the time goes in v1:
time: 223 us; the launch traced here: 220 us
  Pallas kernels  216 us (97%)
  local copies, waits for them, and re-layouts  4.09 us (2%)
    pallas_call x1, Pallas kernels, local_block(): pl.pallas_call(functools.partial(kernel, nx, ny), out_shape=(pltpu.VMEM((...  216 us

profile of v1, /device:TPU:97, one launch (start us, length us, event | category | flops | bytes accessed | tf_op | source)
XLA Modules:
  0.0 220.1 jit_solution(546193411831471475)
XLA Ops:
  0.0 216.0 %shard_map.28 = (bf16[1024,5120]{1,0:T(8,128)(2,1)S(1)}, bf16[8,4,640,1280]{3,2,1,0:T(8,128)(2,1)}) custom-call(bf16[4096,1280]{1,0:T(8,128)(2,1)} %a_ref.1, bf16[640,1280]{1,0:T(8,128)(2,1)} %b_ref.1), custom_call_target="tpu_custom_call" | custom-call | tf_op jit(solution)/shard_map/pallas_call | solution.py:313
  216.0 4.1 %copy.4 = bf16[1024,5120]{1,0:T(8,128)(2,1)} copy(bf16[1024,5120]{1,0:T(8,128)(2,1)S(1)} %get-tuple-element.6) | data formatting | bytes 20971520

commit v2 on v1

--- a/solution.py
+++ b/solution.py
@@ -13,23 +13,44 @@
 FIRST = 3
 PIECES = ((0, FIRST), (FIRST, PARTS))
 
-_NEAR = [
-    [(0, 0)], [(0, -1)], [(1, -1)], [(2, 0)], [(2, -1)], [(0, 1), (2, 1)], [(0, 2), (2, 2)], [(-1, -1)],
-    [(1, 0), (-1, 0)], [(1, 2), (-1, 2)], [(1, 1), (-1, 1)],
-]
-_FAR = [
-    [(1, 0)], [(1, -1)], [(0, -1)], [(-1, 0)], [(-1, -1)], [(1, 1), (-1, 1)], [(1, 2), (-1, 2)], [(2, -1)],
-    [(0, 0), (2, 0)], [(0, 2), (2, 2)], [(0, 1), (2, 1)],
-]
-_FINAL = (21, 23, 25, 27, 28, 29, 30, 31)
-
-_EVENTS = [((-1, 0), 0), ((1, 0), 0), ((0, -1), 0), ((0, 1), 0), ((-1, 0), 1), ((1, 0), 1), ((0, -1), 1), ((0, 1), 1), ((-1, -1), 0), ((-1, 1), 0), ('T', 0), ((-1, -1), 1), ((-1, 1), 1), ('T', 1), ((-1, 2), 0), ((1, 1), 0), ('L', 0), ((2, 0), 0), ((-1, 2), 1), ((1, 1), 1), ((2, 0), 1), ('U', 0), ((1, -1), 0), ((2, 1), 0), ('E', 0), ('U', 1), ((1, -1), 1), ((2, 1), 1), ((2, -1), 0), ((2, -1), 1), ('Z', 0), ((0, 2), 0), ((2, 2), 0), ((0, 2), 1), ((1, 2), 0), ((2, 2), 1), ((1, 2), 1)]
-_COUNTS = [17, 0, 0, 0, 0, 3, 6, 0, 2, 0, 0, 0, 0, 1, 0, 0, 1, 0, 1, 0, 1, 0, 2, 0, 0, 0, 2, 1, 0, 0, 0, 0]
-_FRESH = (0, 5, 6, 16, 18, 20, 22, 26)
+_KINDS = (-1, 0, 1, 2, "side", "far")
+
+
+def _unit(code):
+    return _KINDS[code // 8], code // 2 % 4 - 1, code % 2
+
+
+def _event(code):
+    if isinstance(code, str):
+        return code[0], len(code) - 1
+    return (code // 8 - 1, code // 2 % 4 - 1), code % 2
+
+
+_NEAR = [_unit(code) for code in (
+    8, 10, 9, 17, 16, 11, 24, 27, 13, 25, 29, 26, 12, 14, 30, 28,
+    15, 31, 1, 34, 0, 20, 38, 4, 35, 39, 21, 46, 5, 42, 43, 47,
+)]
+_FAR = [_unit(code) for code in (
+    19, 9, 8, 17, 16, 18, 0, 1, 4, 2, 5, 21, 3, 22, 20, 6,
+    23, 7, 25, 38, 24, 12, 34, 28, 39, 13, 35, 46, 29, 42, 43, 47,
+)]
+
+_EVENTS = [_event(code) for code in (
+    2, 12, 9, 18, 13, 19, "T", 3, 0, 1, "TT", 6, 26, 8, "L", 5,
+    4, 7, 27, 16, "U", 28, 20, 21, "E", 17, "UU", 24, 29, 25, "Z", 22,
+    23, 30, 14, 15, 31,
+)]
+_COUNTS = [17, 2, 0, 0, 1, 1, 4, 0, 1, 0, 1, 0, 2, 0, 0, 0, 1, 1, 1, 0, 0, 0, 0, 1, 1, 0, 2, 0, 1, 0, 0, 0]
+_FRESH = (0, 1, 6, 8, 16)
 
 
 def order(table):
-    return [(k, i, h) for row in table for h in range(2) for k, i in row]
+    return table
+
+
+def is_last(unit, near):
+    k, i, _ = unit
+    return k == "far" or (i == 1 and k in ((1, -1) if near else (0, 2)))
 
 
 def plan():
@@ -66,15 +87,17 @@
     if what == (2, 0):
         out = [("y", -1, what, h)]
         if h:
-            out += [("y", 1, b, q) for b in ((2, 0), (0, -1)) for q in range(2)]
+            out += [("y", 1, what, q) for q in range(2)]
     if what == (-1, -1):
         out = [("y", 1, what, h)]
         if h:
-            out += [("y", 1, b, q) for b in ((1, 0),) for q in range(2)]
-    if what == (1, -1) and h == 0:
+            out += [("y", 1, (1, 0), q) for q in range(2)]
+    if what == (1, -1):
         out = [("y", 1, what, h)]
-    if what == (0, 2) and h == 1:
-        out = [("x", -1, what, h)]
+        if h:
+            out += [("y", 1, (0, -1), 0)]
+    if what == (2, -1) and h:
+        out = out + [("x", -1, (-1, 2), 1)]
     return out + [("c", 1, what, h)]
 
 
@@ -211,36 +234,60 @@
         copy.wait()
     own_a.wait()
 
-    codes = [[(k + 1) * 8 + (i + 1) * 2 + h for k, i, h in order(t)] for t in (_NEAR, _FAR)]
-    per = 6
-    pack = lambda t, w: sum(v * 32 ** n for n, v in enumerate(t[w * per:(w + 1) * per]))
-    words = [jnp.where(near, pack(codes[0], w), pack(codes[1], w)) for w in range(-(-len(codes[0]) // per))]
-
-    def unit(s):
+    def unit(t):
+        both = []
+        for table, is_near in ((_FAR, False), (_NEAR, True)):
+            k, i, h = order(table)[t]
+            if isinstance(k, str):
+                shift = ny // 2
+                row = lax.rem(y + shift, ny)
+                if k == "side":
+                    row = lax.rem(y + 1 - 2 * lax.rem(y, 2) + shift, ny)
+                fields = (row, row + ny, lax.rem(x + i, nx))
+            else:
+                k = xs(k)
+                ro = lax.div(k, nx // 2)
+                fields = (2 * k, 2 * k + 1, lax.rem(x + i * (1 - 2 * ro) + 2 * nx, nx))
+            both.append(fields + (h, int(is_last(order(table)[t], is_near))))
+        return [jnp.where(near, v, u) for u, v in zip(*both)]
+
+    base, per = 1024, 3
+    words = []
+    for t in range(len(_COUNTS)):
+        r1, r2, n, h, final = unit(t)
+        code = (r1 + 8 * r2 + 64 * n + 256 * h + 512 * final) * base ** (t % per)
+        if t % per:
+            words[-1] += code
+        else:
+            words.append(code)
+
+    def decode(s):
         w, m = lax.div(s, per), lax.rem(s, per)
         word = words[0]
         for n in range(1, len(words)):
             word = jnp.where(w == n, words[n], word)
-        code = lax.rem(word, 32)
+        code = word
         for n in range(1, per):
-            code = jnp.where(m == n, lax.rem(lax.div(word, 32 ** n), 32), code)
-        k = xs(lax.div(code, 8) - 1)
-        ro = lax.div(k, nx // 2)
-        n = lax.rem(x + (lax.div(lax.rem(code, 8), 2) - 1) * (1 - 2 * ro) + 2 * nx, nx)
-        return k, ro, n, lax.rem(code, 2)
-
-    def fetch(s, what, start):
-        k, ro, n, h = what
+            code = jnp.where(m == n, lax.div(word, base ** n), code)
+        code = lax.rem(code, base)
+        out = []
+        for size in (8, 8, 4, 2, 2):
+            out.append(lax.rem(code, size))
+            code = lax.div(code, size)
+        return tuple(out)
+
+    def fetch(s, this, start):
+        n, h = this[2], this[3]
         p = lax.rem(s, 2)
         for hh in range(2):
             @pl.when(h == hh)
             def _():
                 for q in range(2):
-                    r = 2 * k + q
+                    r = this[q]
                     copy = pltpu.make_async_copy(
                         piece(r, n, hh), bbuf.at[p, pl.ds(q * kb, kb), pl.ds(0, cols(hh).size)], load_sem.at[p, q])
                     if start:
-                        @pl.when(ro != c)
+                        @pl.when(lax.div(r, ny) != c)
                         def _():
                             wait_b(r, n, hh)
                         copy.start()
@@ -251,10 +298,13 @@
     ahead = [t for t in range(1, len(steps)) if t not in _FRESH]
 
     def is_in(s, those):
-        hit = s == -1
-        for t in those:
+        hit = s == those[0]
+        for t in those[1:]:
             hit = jnp.logical_or(hit, s == t)
         return hit
+
+    def rows_of_a(r):
+        return av[lax.div(r, 2), :, pl.ds(pl.multiple_of(lax.rem(r, 2) * kb, 128), kb)]
 
     def step(s, this):
         for t, events in enumerate(steps):
@@ -264,36 +314,36 @@
                     for event in events:
                         handle(event)
 
-        @pl.when(jnp.logical_not(is_in(s, ahead)))
+        @pl.when(is_in(s, _FRESH))
         def _():
             fetch(s, this, True)
 
-        after = unit(s + 1)
-
-        @pl.when(is_in(s + 1, ahead))
+        after = decode(s + 1)
+
+        @pl.when(jnp.logical_not(is_in(s, [t - 1 for t in _FRESH if t] + [len(steps) - 1])))
         def _():
             fetch(s + 1, after, True)
 
         fetch(s, this, False)
-        k, _, n, h = this
+        r1, r2, n, h, final = this
         p = lax.rem(s, 2)
-        final = is_in(s, _FINAL)
         for hh, (first, last) in enumerate(PIECES):
             @pl.when(h == hh)
             def _():
                 for g in range(first, last):
                     col = n * PARTS + g
+                    lhs = jnp.concatenate([rows_of_a(r1), rows_of_a(r2)], axis=1)
                     acc[col] += jnp.dot(
-                        av[k], bbuf[p, :, pl.ds((g - first) * part, part)], preferred_element_type=jnp.float32)
-
-                @pl.when(final)
+                        lhs, bbuf[p, :, pl.ds((g - first) * part, part)], preferred_element_type=jnp.float32)
+
+                @pl.when(final == 1)
                 def _():
                     for g in range(first, last):
                         col = n * PARTS + g
                         o_ref[:, pl.ds(pl.multiple_of(col * part, part), part)] = acc[col].astype(o_ref.dtype)
         return after
 
-    lax.fori_loop(0, len(steps), step, unit(0))
+    lax.fori_loop(0, len(steps), step, decode(0))
     for n, (_, _, what, h) in enumerate(sent):
         ref = piece(0, 0, h) if not isinstance(what, str) else av.at[0] if what in "LH" else transit.at[0]
         wait(ref, send_sem.at[n])

time: 223 us -> 214 us (0.960); the launches traced: 220 us -> 214 us
  Pallas kernels: 216 us -> 209 us
    pallas_call x1, Pallas kernels: 216 us -> 209 us  [local_block(): pl.pallas_call(functools.partial(kernel, nx, ny), out_shape=(pltpu.VMEM((...]
where the time goes in v2:
time: 214 us
  Pallas kernels  209 us (98%)
  local copies, waits for them, and re-layouts  4.09 us (2%)
    pallas_call x1, Pallas kernels, local_block(): pl.pallas_call(functools.partial(kernel, nx, ny), out_shape=(pltpu.VMEM((...  209 us

profile of v2, /device:TPU:97, one launch (start us, length us, event | category | flops | bytes accessed | tf_op | source)
XLA Modules:
  0.0 213.6 jit_solution(16587864638762181828)
XLA Ops:
  0.0 209.5 %shard_map.28 = (bf16[1024,5120]{1,0:T(8,128)(2,1)S(1)}, bf16[8,4,640,1280]{3,2,1,0:T(8,128)(2,1)}) custom-call(bf16[4096,1280]{1,0:T(8,128)(2,1)} %a_ref.1, bf16[640,1280]{1,0:T(8,128)(2,1)} %b_ref.1), custom_call_target="tpu_custom_call" | custom-call | tf_op jit(solution)/shard_map/pallas_call | solution.py:363
  209.5 4.1 %copy.4 = bf16[1024,5120]{1,0:T(8,128)(2,1)} copy(bf16[1024,5120]{1,0:T(8,128)(2,1)S(1)} %get-tuple-element.6) | data formatting | bytes 20971520

commit v3 on v2

--- a/solution.py
+++ b/solution.py
@@ -27,21 +27,21 @@
 
 
 _NEAR = [_unit(code) for code in (
-    8, 10, 9, 17, 16, 11, 24, 27, 13, 25, 29, 26, 12, 14, 30, 28,
-    15, 31, 1, 34, 0, 20, 38, 4, 35, 39, 21, 46, 5, 42, 43, 47,
+    8, 16, 17, 9, 10, 25, 11, 12, 29, 27, 26, 24, 28, 30, 14, 13,
+    31, 15, 39, 38, 0, 34, 4, 35, 20, 1, 5, 46, 21, 47, 42, 43,
 )]
 _FAR = [_unit(code) for code in (
-    19, 9, 8, 17, 16, 18, 0, 1, 4, 2, 5, 21, 3, 22, 20, 6,
-    23, 7, 25, 38, 24, 12, 34, 28, 39, 13, 35, 46, 29, 42, 43, 47,
+    9, 16, 19, 8, 17, 0, 18, 3, 1, 21, 2, 4, 20, 5, 6, 22,
+    23, 7, 25, 35, 34, 24, 12, 28, 38, 39, 13, 46, 29, 47, 42, 43,
 )]
 
 _EVENTS = [_event(code) for code in (
-    2, 12, 9, 18, 13, 19, "T", 3, 0, 1, "TT", 6, 26, 8, "L", 5,
-    4, 7, 27, 16, "U", 28, 20, 21, "E", 17, "UU", 24, 29, 25, "Z", 22,
-    23, 30, 14, 15, 31,
+    2, 3, 18, 19, 5, "T", 4, 0, 1, "TT", 13, 6, 8, 9, 12, "L",
+    7, 26, 21, 27, 20, "E", 16, "U", 17, "UU", 28, 24, 29, 25, "Z", 22,
+    23, 30, 31, 14, 15,
 )]
-_COUNTS = [17, 2, 0, 0, 1, 1, 4, 0, 1, 0, 1, 0, 2, 0, 0, 0, 1, 1, 1, 0, 0, 0, 0, 1, 1, 0, 2, 0, 1, 0, 0, 0]
-_FRESH = (0, 1, 6, 8, 16)
+_COUNTS = [18, 1, 1, 0, 1, 2, 1, 1, 1, 1, 0, 0, 1, 0, 2, 0, 0, 1, 0, 1, 0, 0, 0, 0, 2, 0, 0, 2, 1, 0, 0, 0]
+_FRESH = (0, 5)
 
 
 def order(table):
@@ -95,9 +95,9 @@
     if what == (1, -1):
         out = [("y", 1, what, h)]
         if h:
-            out += [("y", 1, (0, -1), 0)]
-    if what == (2, -1) and h:
-        out = out + [("x", -1, (-1, 2), 1)]
+            out += [("y", 1, (0, -1), 0), ("y", 1, (0, -1), "q")]
+    if what == (1, 2) and h:
+        out = out + [("x", -1, (-1, 2), "t")]
     return out + [("c", 1, what, h)]
 
 
@@ -108,7 +108,7 @@
 
 
 def kernel(nx, ny, a_ref, b_ref, o_ref, bg, av, transit, acc, bbuf,
-           a_load, b_load, load_sem, recv_b, recv_a, send_sem):
+           a_load, b_load, load_sem, recv_b, recv_q, recv_a, send_sem):
     x, y, c = lax.axis_index("co"), lax.axis_index("ri"), lax.axis_index("ro")
     d = 1 - 2 * c
     xs = lambda i: lax.rem(x + i * d + 2 * nx, nx)
@@ -134,6 +134,13 @@
 
     def a_rows(s, first, count):
         return a_ref.at[pl.ds(pl.multiple_of(xs(s) * rows + first, half), count)]
+
+    def rows_piece(r, n, h):
+        if h == "q":
+            return bg.at[r, n, pl.ds(0, kb // 4), cols(1)]
+        if h == "t":
+            return bg.at[r, n, pl.ds(kb // 4, kb - kb // 4), cols(1)]
+        return piece(r, n, h)
 
     sent = []
 
@@ -156,9 +163,9 @@
         else:
             i, j = what
             r, n = row_of(j), xs(i)
-            dst = piece(r, n, h)
+            dst = rows_piece(r, n, h)
             src = b_ref.at[:, cols(h)] if what == (0, 0) else dst
-            sems = send_sem.at[index], recv_b.at[r, n, h]
+            sems = send_sem.at[index], recv_q if h == "q" else recv_b.at[r, n, 1 if h == "t" else h]
         pltpu.make_async_remote_copy(
             src_ref=src, dst_ref=dst, send_sem=sems[0], recv_sem=sems[1],
             device_id=target(axis, s), device_id_type=MESH).start()
@@ -197,7 +204,12 @@
             only(what == "Z", wait_behind)
         else:
             i, j = what
-            wait_b(row_of(j), xs(i), h)
+            if what == (0, 2) and h:
+                r, n = row_of(j), xs(i)
+                wait(rows_piece(r, n, "q"), recv_q)
+                wait(rows_piece(r, n, "t"), recv_b.at[r, n, h])
+            else:
+                wait_b(row_of(j), xs(i), h)
         both = [sends(event, want) for want in (False, True)]
         if both[0] == both[1]:
             for send in both[0]:
@@ -345,7 +357,7 @@
 
     lax.fori_loop(0, len(steps), step, decode(0))
     for n, (_, _, what, h) in enumerate(sent):
-        ref = piece(0, 0, h) if not isinstance(what, str) else av.at[0] if what in "LH" else transit.at[0]
+        ref = rows_piece(0, 0, h) if not isinstance(what, str) else av.at[0] if what in "LH" else transit.at[0]
         wait(ref, send_sem.at[n])
 
 
@@ -374,7 +386,7 @@
                 pltpu.VMEM((nx * PARTS, rows, part), jnp.float32),
                 pltpu.VMEM((2, 2 * kb, FIRST * part), jnp.bfloat16),
                 dma, dma((2,)), dma((2, 2)),
-                dma((nc * ny, nx, 2)), dma((6,)), dma((len(all_sends),)),
+                dma((nc * ny, nx, 2)), dma, dma((6,)), dma((len(all_sends),)),
             ],
             compiler_params=pltpu.CompilerParams(
                 collective_id=0, has_side_effects=True, vmem_limit_bytes=VMEM),

time: 214 us -> 212 us (level)
  no operation moved by 1% of the time
where the time goes in v3:
time: 212 us
  Pallas kernels  208 us (98%)
  local copies, waits for them, and re-layouts  4.09 us (2%)
    pallas_call x1, Pallas kernels, local_block(): pl.pallas_call(functools.partial(kernel, nx, ny), out_shape=(pltpu.VMEM((...  208 us

profile of v3, /device:TPU:97, one launch (start us, length us, event | category | flops | bytes accessed | tf_op | source)
XLA Modules:
  0.0 211.6 jit_solution(8306248220723532304)
XLA Ops:
  0.0 207.5 %shard_map.28 = (bf16[1024,5120]{1,0:T(8,128)(2,1)S(1)}, bf16[8,4,640,1280]{3,2,1,0:T(8,128)(2,1)}) custom-call(bf16[4096,1280]{1,0:T(8,128)(2,1)} %a_ref.1, bf16[640,1280]{1,0:T(8,128)(2,1)} %b_ref.1), custom_call_target="tpu_custom_call" | custom-call | tf_op jit(solution)/shard_map/pallas_call | solution.py:375
  207.5 4.1 %copy.4 = bf16[1024,5120]{1,0:T(8,128)(2,1)} copy(bf16[1024,5120]{1,0:T(8,128)(2,1)S(1)} %get-tuple-element.6) | data formatting | bytes 20971520

commit v4 on v3

--- a/solution.py
+++ b/solution.py
@@ -340,19 +340,21 @@
         r1, r2, n, h, final = this
         p = lax.rem(s, 2)
         for hh, (first, last) in enumerate(PIECES):
-            @pl.when(h == hh)
+            def total(g, first=first):
+                lhs = jnp.concatenate([rows_of_a(r1), rows_of_a(r2)], axis=1)
+                rhs = bbuf[p, :, pl.ds((g - first) * part, part)]
+                return acc[n * PARTS + g] + jnp.dot(lhs, rhs, preferred_element_type=jnp.float32)
+
+            @pl.when(jnp.logical_and(h == hh, final == 0))
             def _():
                 for g in range(first, last):
-                    col = n * PARTS + g
-                    lhs = jnp.concatenate([rows_of_a(r1), rows_of_a(r2)], axis=1)
-                    acc[col] += jnp.dot(
-                        lhs, bbuf[p, :, pl.ds((g - first) * part, part)], preferred_element_type=jnp.float32)
-
-                @pl.when(final == 1)
-                def _():
-                    for g in range(first, last):
-                        col = n * PARTS + g
-                        o_ref[:, pl.ds(pl.multiple_of(col * part, part), part)] = acc[col].astype(o_ref.dtype)
+                    acc[n * PARTS + g] = total(g)
+
+            @pl.when(jnp.logical_and(h == hh, final == 1))
+            def _():
+                for g in range(first, last):
+                    at = pl.ds(pl.multiple_of((n * PARTS + g) * part, part), part)
+                    o_ref[:, at] = total(g).astype(o_ref.dtype)
         return after
 
     lax.fori_loop(0, len(steps), step, decode(0))

time: 212 us -> 211 us (level)
  no operation moved by 1% of the time
where the time goes in v4:
time: 211 us
  Pallas kernels  207 us (98%)
  local copies, waits for them, and re-layouts  4.09 us (2%)
    pallas_call x1, Pallas kernels, local_block(): pl.pallas_call(functools.partial(kernel, nx, ny), out_shape=(pltpu.VMEM((...  207 us

profile of v4, /device:TPU:97, one launch (start us, length us, event | category | flops | bytes accessed | tf_op | source)
XLA Modules:
  0.0 211.0 jit_solution(10431193195326120704)
XLA Ops:
  0.0 206.9 %shard_map.28 = (bf16[1024,5120]{1,0:T(8,128)(2,1)S(1)}, bf16[8,4,640,1280]{3,2,1,0:T(8,128)(2,1)}) custom-call(bf16[4096,1280]{1,0:T(8,128)(2,1)} %a_ref.1, bf16[640,1280]{1,0:T(8,128)(2,1)} %b_ref.1), custom_call_target="tpu_custom_call" | custom-call | tf_op jit(solution)/shard_map/pallas_call | solution.py:377
  206.9 4.1 %copy.4 = bf16[1024,5120]{1,0:T(8,128)(2,1)} copy(bf16[1024,5120]{1,0:T(8,128)(2,1)S(1)} %get-tuple-element.6) | data formatting | bytes 20971520
